TPU v7x, 32 devices: a whole 2x2x4 slice. The times are simulated.
32 devices in a mesh: band: 8 (over y, x, core), sub: 4 (over z).
Axes of the slice: x: 2, y: 2, z: 4, core: 2. Of those that a mesh axis runs over, the one named last changes fastest.
Arguments:
- gas_amounts: bfloat16 [512, 64, 8, 128], P('band'), may hold values from 0.049804688 to 1
- layer_mass: bfloat16 [512, 64, 128], P('band'), may hold values from 4 to 40
- column_state: bfloat16 [512, 2, 128], P('band'), may hold values from 0.099609375 to 0.796875
- absorption: bfloat16 [112, 8], P('sub'), may hold values from 0.0019989014 to 0.5
- single_scatter: float32 [112], P('sub'), may hold values from 0.2 to 0.95
- solar_weight: float32 [112], P('sub'), may hold values from 0.002 to 0.1
- sunlit: int32 [512], replicated, may hold values from 0 to 1, as said below
Outputs:
- heating: float32 [512, 64, 128], P(('band', 'sub'))
- surface_down: float32 [512, 128], P(('band', 'sub'))
Inputs may be any that keep to these rules, and one draw needn't show every extreme that they name: Exactly 256 blocks are sunlit, and in every draw all 64 blocks of some band index are sunlit.
All inputs are finite; a program needn't handle non-finite values.
Results may differ from a plain program's by a relative error of at most 0.0003.
Values may be sent and summed in bfloat16 or wider, within the bound.
A program may use at most 256 MiB of HBM per device.

v0:
```python
import jax
import jax.numpy as jnp
from jax import lax
from jax.sharding import PartitionSpec as P


def layer_solve(optical, heat_factor, cosine, ground, single_scatter, solar_weight):
    omega = single_scatter[:, None]
    passing = jnp.exp(-optical)
    reflected = 0.5 * omega * (1.0 - passing * passing)
    unscattered = jnp.exp(-optical / cosine[None, None, :])

    def upward(lower_albedo, layer_data):
        reflect_now, pass_now = layer_data
        denominator = 1.0 - reflect_now * lower_albedo
        upper_albedo = reflect_now + pass_now * pass_now * lower_albedo / denominator
        return (upper_albedo, (upper_albedo, denominator))

    surface = jnp.broadcast_to(ground[None, :], optical.shape[1:])
    _, (stack_albedo, denominators) = lax.scan(
        upward, surface, (reflected, passing), reverse=True, unroll=8
    )

    def downward(state_now, layer_data):
        beam, diffuse = state_now
        albedo_now, pass_now, direct_now, denominator = layer_data
        net_flux = (1.0 - albedo_now) * (beam + diffuse)
        new_beam = beam * direct_now
        new_diffuse = (pass_now * diffuse + 0.5 * omega * (1.0 - direct_now) * beam) / denominator
        return ((new_beam, new_diffuse), jnp.sum(net_flux, axis=0))

    top_beam = solar_weight[:, None] * cosine[None, :]
    (beam, diffuse), net_sums = lax.scan(
        downward,
        (top_beam, jnp.zeros_like(top_beam)),
        (stack_albedo, passing, unscattered, denominators),
        unroll=8,
    )
    bottom_down = beam + diffuse
    bottom_net = jnp.sum((1.0 - ground[None, :]) * bottom_down, axis=0)
    interfaces = jnp.concatenate([net_sums, bottom_net[None, :]], axis=0)
    heating = heat_factor * (interfaces[:-1] - interfaces[1:])
    return (heating, jnp.sum(bottom_down, axis=0))


def pick_rows(array, index, lead_shape):
    return jnp.take(array, index, axis=0).reshape(lead_shape + array.shape[1:])


def compact(arrived, flat_slot):
    return jnp.take(
        arrived.reshape((arrived.shape[0] * arrived.shape[1],) + arrived.shape[2:]),
        flat_slot,
        axis=0,
    )


def body(gas_amounts, layer_mass, column_state, absorption, single_scatter, solar_weight, sunlit):
    band_count = lax.axis_size("band")
    sub_count = lax.axis_size("sub")
    band_index = lax.axis_index("band")
    sub_index = lax.axis_index("sub")
    owned, levels, gas_count, columns = gas_amounts.shape
    capacity = (owned + band_count - 1) // band_count
    helped = owned // 2
    before = jnp.cumsum(sunlit) - sunlit
    starts = before.reshape(band_count, owned)[:, 0]
    sunlit_mine = lax.dynamic_slice_in_dim(sunlit, band_index * owned, owned)
    my_rank = lax.dynamic_slice_in_dim(before, band_index * owned, owned)
    first_rank = starts[band_index]
    local_pos = my_rank - first_rank
    band_ids = jnp.arange(band_count, dtype=jnp.int32)
    block_ids = jnp.arange(owned, dtype=jnp.int32)
    per_dest = (capacity + sub_count - 1) // sub_count
    share = helped // sub_count
    lead_send = (band_count, per_dest)

    def first_turn(start_rank, dest):
        lowest = (start_rank - dest + band_count - 1) // band_count
        return lowest + jnp.mod(sub_index - lowest, sub_count)

    my_turn = first_turn(first_rank, band_ids)
    turns = my_turn[:, None] + jnp.arange(per_dest, dtype=jnp.int32)[None, :] * sub_count
    wanted = (turns * band_count + band_ids[:, None] - first_rank).reshape(-1)
    matches = (sunlit_mine[None, :] == 1) & (local_pos[None, :] == wanted[:, None])
    source_block = jnp.sum(jnp.where(matches, block_ids[None, :], 0), axis=1)
    arrived_gas, arrived_mass, arrived_state = (
        lax.all_to_all(
            pick_rows(gas_amounts, source_block, lead_send),
            "band",
            split_axis=0,
            concat_axis=0,
            tiled=True,
        ),
        lax.all_to_all(
            pick_rows(layer_mass, source_block, lead_send),
            "band",
            split_axis=0,
            concat_axis=0,
            tiled=True,
        ),
        lax.all_to_all(
            pick_rows(column_state, source_block, lead_send),
            "band",
            split_axis=0,
            concat_axis=0,
            tiled=True,
        ),
    )
    helper_turn = sub_index + jnp.arange(share, dtype=jnp.int32) * sub_count
    sender = (
        jnp.sum(
            (starts[None, :] <= (helper_turn * band_count + band_index)[:, None]).astype(jnp.int32),
            axis=1,
        )
        - 1
    )
    flat_slot = (
        sender * per_dest + (helper_turn - first_turn(starts[sender], band_index)) // sub_count
    )
    got_gas = compact(arrived_gas, flat_slot)
    got_mass = compact(arrived_mass, flat_slot)
    got_state = compact(arrived_state, flat_slot)
    table_all, omega_all, weight_all = (
        lax.all_gather(absorption.astype(jnp.float32), "sub", axis=0, tiled=True),
        lax.all_gather(single_scatter, "sub", axis=0, tiled=True),
        lax.all_gather(solar_weight, "sub", axis=0, tiled=True),
    )
    coefficients = table_all.astype(jnp.bfloat16)
    back_turn = (
        first_turn(starts, band_index)[:, None]
        + jnp.arange(per_dest, dtype=jnp.int32)[None, :] * sub_count
    )
    help_slot = jnp.clip((back_turn - sub_index) // sub_count, 0, share - 1).reshape(-1)
    own_dest = jnp.mod(my_rank, band_count)
    own_turn = my_rank // band_count
    own_first = jnp.sum(
        jnp.where(band_ids[None, :] == own_dest[:, None], my_turn[None, :], 0), axis=1
    )
    own_slot = jnp.clip(
        own_dest * per_dest + (own_turn - own_first) // sub_count, 0, band_count * per_dest - 1
    )
    own_keep = (sunlit_mine == 1) & (jnp.mod(own_turn, sub_count) == sub_index)
    solved = got_gas.shape[0]
    gpoint_share = coefficients.shape[0]
    optical = jnp.einsum("gs,plsc->lgpc", coefficients, got_gas, preferred_element_type=jnp.float32)
    optical = optical.reshape(levels, gpoint_share, solved * columns)
    heat_factor = (
        jnp.transpose(got_mass, (1, 0, 2)).reshape(levels, solved * columns).astype(jnp.float32)
    )
    cosine = got_state[:, 0, :].reshape(-1).astype(jnp.float32)
    ground = got_state[:, 1, :].reshape(-1).astype(jnp.float32)
    heating, surface_down = layer_solve(optical, heat_factor, cosine, ground, omega_all, weight_all)
    heating = jnp.transpose(heating.reshape(levels, solved, columns), (1, 0, 2))
    surface_down = surface_down.reshape(solved, columns)
    lead_back = (band_count, per_dest)
    heat_back, surface_back = (
        lax.all_to_all(
            pick_rows(heating, help_slot, lead_back),
            "band",
            split_axis=0,
            concat_axis=0,
            tiled=True,
        ),
        lax.all_to_all(
            pick_rows(surface_down, help_slot, lead_back),
            "band",
            split_axis=0,
            concat_axis=0,
            tiled=True,
        ),
    )
    heat_own = compact(heat_back, own_slot)
    surface_own = compact(surface_back, own_slot)
    heat_own = jnp.where(own_keep[:, None, None], heat_own, jnp.zeros_like(heat_own))
    surface_own = jnp.where(own_keep[:, None], surface_own, jnp.zeros_like(surface_own))
    heating_out, surface_out = (
        lax.psum_scatter(heat_own, "sub", scatter_dimension=0, tiled=True),
        lax.psum_scatter(surface_own, "sub", scatter_dimension=0, tiled=True),
    )
    return (heating_out, surface_out)


def solution(mesh):
    in_specs = (
        P("band", None, None, None),
        P("band", None, None),
        P("band", None, None),
        P("sub", None),
        P("sub"),
        P("sub"),
        P(),
    )
    out_specs = (P(("band", "sub"), None, None), P(("band", "sub"), None))
    return jax.shard_map(body, mesh=mesh, in_specs=in_specs, out_specs=out_specs, check_vma=False)
```

profile of v0, /device:TPU:2, one launch (start us, length us, event | category | flops | bytes accessed | tf_op | source)
XLA Modules:
  0.0 537.3 jit_solution(2903076316715447955)
XLA Ops:
  20.1 4.3 gather_fusion.5
  33.1 5.3 all-to-all-done
  38.4 5.0 all-to-all-start.2
  43.4 12.2 %all-gather = bf16[4,28,8]{1,2,0:T(8,128)(2,1)S(1)} all-gather(bf16[1,28,8]{1,2,0:T(8,128)(2,1)S(1)} %bitcast.569), channel_id=1, replica_groups=mesh['band'=8,'sub'=4] {'sub'}, dimensions={0}, use_global_device_ids=true | all-gather | bytes 2240 | tf_op jit(solution)/shard_map/all_gather | solution.py:125
  57.4 10.6 %all-reduce.2 = (f32[112]{0:T(128)S(1)}, f32[112]{0:T(128)S(1)}) all-reduce(f32[112]{0:T(128)S(1)} %dynamic-update-slice, f32[112]{0:T(128)S(1)} %dynamic-update-slice.1), channel_id=1, replica_groups=mesh['band'=8,'sub'=4] {'sub'}, use_global_device_ids=true, to_apply=%add | all-reduce | flops 224 | bytes 1792
  74.1 11.6 %negate_bitcast_fusion = f32[64,112,8,128]{3,1,0,2:T(8,128)} fusion(bf16[8,64,8,128]{3,2,1,0:T(8,128)(2,1)S(1)} %gather_fusion.6, pred[8]{0:T(512)(128)(4,1)S(1)} %compare_and_fusion.2, bf16[112,8,1,1]{0,1,2,3:T(8,128)(2,1)S(1)} %reshape.776), kind=kOutput, calls=%fused_computation.177 | convolution fusion | flops 125304832 | bytes 30410504 | tf_op jit(solution)/shard_map/gs,plsc->lgpc/dot_general | solution.py:146
  85.7 28.5 %copy.54 = f32[64,112,8,128]{3,2,1,0:T(8,128)} copy(f32[64,112,8,128]{3,1,0,2:T(8,128)} %negate_bitcast_fusion) | data formatting | bytes 58720256 | tf_op jit(solution)/shard_map/neg | solution.py:9
  114.3 31.1 %neg.15 = f32[8,8,112,1024]{3,2,1,0:T(8,128)} reshape(f32[64,112,8,128]{3,2,1,0:T(8,128)} %copy.54) | data formatting | bytes 58720256 | tf_op jit(solution)/shard_map/neg | solution.py:9
  145.4 39.1 %subtract_multiply_fusion = (f32[8,8,112,1024]{3,2,1,0:T(8,128)}, f32[8,8,112,1024]{3,2,1,0:T(8,128)}, f32[8,8,112,1024]{3,2,1,0:T(8,128)}) fusion(f32[112]{0:T(128)S(1)} %broadcast_multiply_fusion.1, f32[8,8,112,1024]{3,2,1,0:T(8,128)} %neg.15, f32[1024]{0:T(1024)S(1)} %bitcast.561), kind=kLoop, calls=%fused_computation.175 | loop fusion | flops 29360128 | bytes 117445056 | tf_op jit(solution)/shard_map/mul | solution.py:10
  184.5 13.5 %broadcast.869 = f32[8,8,112,1024]{3,2,1,0:T(8,128)} broadcast(f32[]{:T(128)} %constant.345.clone.1), dimensions={} | broadcast | bytes 29360132 | tf_op jit(solution)/shard_map/broadcast.91
  198.0 13.4 %broadcast.869.clone = f32[8,8,112,1024]{3,2,1,0:T(8,128)} broadcast(f32[]{:T(128)} %constant.345.clone.1), dimensions={} | broadcast | bytes 29360132 | tf_op jit(solution)/shard_map/broadcast.91
  211.4 134.7 %while.33 = (s32[]{:T(128)}, f32[112,1024]{1,0:T(8,128)S(1)}, f32[8,8,112,1024]{3,2,1,0:T(8,128)}, f32[8,8,112,1024]{3,2,1,0:T(8,128)}, f32[8,8,112,1024]{3,2,1,...) while((s32[]{:T(128)}, f32[112,1024]{1,0:T(8,128)S(1)}, ...), condition=%wide.region_6.7_spmd, body=%wide.region_5.6_spmd.sunk | while | flops 7340040 | bytes 44040528 | solution.py:20
  240.7 4.3 bitcast_dynamic-update-slice_fusion.51
  257.5 4.6 bitcast_dynamic-update-slice_fusion.51
  274.4 4.4 bitcast_dynamic-update-slice_fusion.51
  291.2 4.4 bitcast_dynamic-update-slice_fusion.51
  308.1 4.4 bitcast_dynamic-update-slice_fusion.51
  324.9 4.4 bitcast_dynamic-update-slice_fusion.51
  341.8 4.3 bitcast_dynamic-update-slice_fusion.51
  346.2 102.9 %while.34 = (s32[]{:T(128)}, f32[112,1024]{1,0:T(8,128)S(1)}, f32[112,1024]{1,0:T(8,128)S(1)}, f32[8,8,1024]{2,1,0:T(8,128)}, f32[8,8,112,1024]{3,2,1,0:T(8,128)...) while((s32[]{:T(128)}, f32[112,1024]{1,0:T(8,128)S(1)}, ...), condition=%wide.region_16.17_spmd.clone, body=%wide.region_7.16_spmd.clone.sunk | while | flops 10199162 | bytes 27233732 | solution.py:33
  349.1 4.5 fusion.149
  362.0 4.4 fusion.149
  374.8 4.5 fusion.149
  387.8 4.4 fusion.149
  400.6 4.4 fusion.149
  413.4 4.4 fusion.149
  426.2 4.4 fusion.149
  439.1 4.4 fusion.149
  459.9 4.9 all-to-all-start.3
  466.2 6.8 %all-to-all-done.3 = f32[8,2,64,128]{3,2,1,0:T(8,128)S(1)} async-done(((f32[8,2,64,128]{3,2,1,0:T(8,128)}), f32[8,2,64,128]{3,2,1,0:T(8,128)S(1)}, u32[]{:S(2)}, u32[]{:S(2)}) %all-to-all-start.3) | async-done | bytes 524320 | tf_op jit(solution)/shard_map/all_to_all | solution.py:158
  478.3 7.4 %reduce-scatter.5.cloned.1.call-done = f32[16,128]{1,0:T(8,128)} async-done(((f32[64,128]{1,0:T(8,128)}), f32[16,128]{1,0:T(8,128)}) %reduce-scatter.5.cloned.1.call-update) | async-done | bytes 8208 | tf_op jit(solution)/shard_map/reduce_scatter | solution.py:179
  485.7 44.7 %reduce-scatter.3.cloned.1.call-done = f32[16,64,128]{2,1,0:T(8,128)} async-done(((f32[64,64,128]{2,1,0:T(8,128)}), f32[16,64,128]{2,1,0:T(8,128)}) %reduce-scatter.3.cloned.1.call-update) | async-done | bytes 524304 | tf_op jit(solution)/shard_map/reduce_scatter | solution.py:178
  (291 shorter events, 216.4 us)
Async XLA Ops:
  7.2 20.0 %copy-start = (bf16[64,64,128]{2,1,0:T(8,128)(2,1)S(1)}, bf16[64,64,128]{2,1,0:T(8,128)(2,1)}, u32[]{:S(2)}) copy-start(bf16[64,64,128]{2,1,0:T(8,128)(2,1)} %param.12) | copy-start | bytes 3145732
  12.7 20.4 %copy-start.12 = (s32[64]{0:T(128)}, s32[64]{0:T(128)S(1)}, u32[]{:S(2)}) copy-start(s32[64]{0:T(128)S(1)} %get-tuple-element.276) | copy-start | bytes 772
  15.8 13.0 %all-to-all-start.1 = ((bf16[8,2,2,128]{3,2,1,0:T(2,128)(2,1)}), bf16[8,2,2,128]{3,2,1,0:T(2,128)(2,1)S(1)}, u32[]{:S(2)}, u32[]{:S(2)}) async-start(bf16[8,2,2,128]{3,2,1,0:T(2,128)(2,1)} %broadcast_select_fusion.3), calls=%async_computation.1 | async-start | bytes 16384 | tf_op jit(solution)/shard_map/all_to_all | solution.py:102
  26.0 17.4 %copy-start.10 = (bf16[28,8]{0,1:T(8,128)(2,1)S(1)}, bf16[28,8]{0,1:T(8,128)(2,1)}, u32[]{:S(2)}) copy-start(bf16[28,8]{0,1:T(8,128)(2,1)} %param.14) | copy-start | bytes 1348
  26.0 29.7 %copy-start.17 = (u32[32]{0:T(128)S(1)}, u32[32]{0:T(128)}, u32[]{:S(2)}) copy-start(u32[32]{0:T(128)} %constant.351) | copy-start | bytes 388
  26.0 30.9 %copy-start.15 = (f32[28]{0:T(128)S(1)}, f32[28]{0:T(128)}, u32[]{:S(2)}) copy-start(f32[28]{0:T(128)} %param.16) | copy-start | bytes 340
  26.1 31.2 %copy-start.16 = (f32[28]{0:T(128)S(1)}, f32[28]{0:T(128)}, u32[]{:S(2)}) copy-start(f32[28]{0:T(128)} %param.15) | copy-start | bytes 340
  28.8 9.6 %all-to-all-start = ((bf16[8,2,64,128]{3,2,1,0:T(8,128)(2,1)}), bf16[8,2,64,128]{3,2,1,0:T(8,128)(2,1)S(1)}, u32[]{:S(2)}, u32[]{:S(2)}) async-start(bf16[8,2,64,128]{3,2,1,0:T(8,128)(2,1)} %broadcast_select_fusion.2), calls=%async_computation | async-start | bytes 524288 | tf_op jit(solution)/shard_map/all_to_all | solution.py:95
  38.4 34.9 %all-to-all-start.2 = ((bf16[8,2,64,8,128]{4,3,2,1,0:T(8,128)(2,1)}), bf16[8,2,64,8,128]{4,3,2,1,0:T(8,128)(2,1)S(1)}, u32[]{:S(2)}, u32[]{:S(2)}) async-start(bf16[8,2,64,8,128]{4,3,2,1,0:T(8,128)(2,1)} %broadcast_select_fusion), calls=%async_computation.2 | async-start | bytes 4194304 | tf_op jit(solution)/shard_map/all_to_all | solution.py:88
  68.0 5.3 copy-start.18
  69.3 16.4 %copy-start.5 = (pred[8]{0:T(512)(128)(4,1)}, pred[8]{0:T(512)(128)(4,1)S(1)}, u32[]{:S(2)}) copy-start(pred[8]{0:T(512)(128)(4,1)S(1)} %compare_and_fusion.2) | copy-start | bytes 28
  211.4 134.7 %copy-start.2 = (f32[112,1024]{1,0:T(8,128)S(1)}, f32[112,1024]{1,0:T(8,128)}, u32[]{:S(2)}) copy-start(f32[112,1024]{1,0:T(8,128)} %broadcast_multiply_fusion) | copy-start | bytes 1376260
  211.4 134.7 %copy-start.3 = (f32[112,1024]{1,0:T(8,128)S(1)}, f32[112,1024]{1,0:T(8,128)}, u32[]{:S(2)}) copy-start(f32[112,1024]{1,0:T(8,128)} %custom-call) | copy-start | bytes 1376260
  211.4 134.7 %copy-start.19 = (f32[112]{0:T(128)S(1)}, f32[112]{0:T(128)}, u32[]{:S(2)}) copy-start(f32[112]{0:T(128)} %copy-done.18) | copy-start | bytes 1348
  346.1 103.0 %copy-start.7 = (f32[1024]{0:T(1024)S(1)}, f32[1024]{0:T(1024)}, u32[]{:S(2)}) copy-start(f32[1024]{0:T(1024)} %broadcast_subtract_fusion) | copy-start | bytes 12292
  346.1 103.0 %copy-start.4 = (bf16[8,64,128]{2,1,0:T(8,128)(2,1)S(1)}, bf16[8,64,128]{2,1,0:T(8,128)(2,1)}, u32[]{:S(2)}) copy-start(bf16[8,64,128]{2,1,0:T(8,128)(2,1)} %gather_fusion.2) | copy-start | bytes 393220
  346.1 103.0 %copy-start.6 = (pred[8]{0:T(512)(128)(4,1)S(1)}, pred[8]{0:T(512)(128)(4,1)}, u32[]{:S(2)}) copy-start(pred[8]{0:T(512)(128)(4,1)} %copy-done.5) | copy-start | bytes 28
  346.1 105.6 %copy-start.8 = (pred[8,2]{1,0:T(8,128)(4,1)S(1)}, pred[8,2]{1,0:T(8,128)(4,1)}, u32[]{:S(2)}) copy-start(pred[8,2]{1,0:T(8,128)(4,1)} %compare_and_fusion.1) | copy-start | bytes 52
  449.0 15.7 %copy-start.11 = (s32[64]{0:T(128)S(1)}, s32[64]{0:T(128)}, u32[]{:S(2)}) copy-start(s32[64]{0:T(128)} %get-tuple-element.275) | copy-start | bytes 772
  449.0 15.7 %copy-start.13 = (s32[64]{0:T(128)S(1)}, s32[64]{0:T(128)}, u32[]{:S(2)}) copy-start(s32[64]{0:T(128)} %copy-done.12) | copy-start | bytes 772
  449.0 15.7 %copy-start.14 = (s32[64]{0:T(128)S(1)}, s32[64]{0:T(128)}, u32[]{:S(2)}) copy-start(s32[64]{0:T(128)} %select_reduce_fusion.1) | copy-start | bytes 772
  449.0 16.4 %copy-start.9 = (pred[64]{0:T(512)(128)(4,1)S(1)}, pred[64]{0:T(512)(128)(4,1)}, u32[]{:S(2)}) copy-start(pred[64]{0:T(512)(128)(4,1)} %get-tuple-element.274) | copy-start | bytes 196
  452.4 7.5 %all-to-all-start.4 = ((f32[8,2,128]{2,1,0:T(2,128)}), f32[8,2,128]{2,1,0:T(2,128)S(1)}, u32[]{:S(2)}, u32[]{:S(2)}) async-start(f32[8,2,128]{2,1,0:T(2,128)} %broadcast_select_fusion.5), calls=%async_computation.5 | async-start | bytes 16384 | tf_op jit(solution)/shard_map/all_to_all | solution.py:165
  459.9 13.1 %all-to-all-start.3 = ((f32[8,2,64,128]{3,2,1,0:T(8,128)}), f32[8,2,64,128]{3,2,1,0:T(8,128)S(1)}, u32[]{:S(2)}, u32[]{:S(2)}) async-start(f32[8,2,64,128]{3,2,1,0:T(8,128)} %broadcast_select_fusion.1), calls=%async_computation.3 | async-start | bytes 1048576 | tf_op jit(solution)/shard_map/all_to_all | solution.py:158
  464.7 21.0 %reduce-scatter.5.cloned.1.call-start = ((), (), s32[]{:S(2)}) async-start(), calls=%async_computation.8 | async-start | bytes 40960 | tf_op jit(solution)/shard_map/reduce_scatter | solution.py:179
  466.1 64.3 %reduce-scatter.3.cloned.1.call-start = ((), (), s32[]{:S(2)}) async-start(), calls=%async_computation.7 | async-start | bytes 2621440 | tf_op jit(solution)/shard_map/reduce_scatter | solution.py:178
  473.0 57.4 %copy-start.1 = (bf16[64,64,128]{2,1,0:T(8,128)(2,1)S(1)}, bf16[64,64,128]{2,1,0:T(8,128)(2,1)}, u32[]{:S(2)}) copy-start(bf16[64,64,128]{2,1,0:T(8,128)(2,1)} %param.12) | copy-start | bytes 3145732
Sparse Core Ops, SparseCore 0:
  468.3 17.3 reduce-scatter.4
  488.6 41.7 reduce-scatter.2
where the time goes:
time: 543 us; the launch traced here: 537 us
  other arithmetic  253 us (47%)
  local copies, waits for them, and re-layouts  145 us (27%)
  waiting for transfers between devices  66.6 us (12%)
  blocking collectives  22.8 us (4%)
  starting transfers between devices  22.6 us (4%)
  between operations  15 us (3%)
  matrix products  11.6 us (2%)
    while x64, other arithmetic  96.9 us
    neg x2, local copies, waits for them, and re-layouts, layer_solve(): passing = jnp.exp(-optical)  59.6 us
    reduce_sum x16, other arithmetic, downward(): return ((new_beam, new_diffuse), jnp.sum(net_flux, axis=0))  49.8 us
    div x16, other arithmetic, downward(): (pass_now * diffuse + 0.5 * omega * (1.0 - direct_now) * beam) / denominator  47.4 us
    reduce_scatter x1, waiting for transfers between devices, body(): lax.psum_scatter(heat_own, 'sub', scatter_dimension=0, tiled=True)  44.7 us
    mul x2, other arithmetic, layer_solve(): reflected = 0.5 * omega * (1.0 - passing * passing)  39.1 us
    dynamic_update_slice x8, local copies, waits for them, and re-layouts, layer_solve(): lax.scan(upward, surface, (reflected, passing), reverse=True, unroll=8)  35.2 us
    another operation x3, local copies, waits for them, and re-layouts  27 us
  transfers between devices with their start and end apart: 7, of which 5 were waited for; matrix products, arithmetic and copies ran while one was open for 4% of the time, Pallas kernels for 0%

commit v1 on v0

v1 whole, which is shorter than its diff:
```python
import functools
import math

import jax
import jax.numpy as jnp
from jax import lax
from jax.experimental import pallas as pl
from jax.experimental.pallas import tpu as pltpu
from jax.sharding import PartitionSpec as P

LOG2E = 1.0 / math.log(2.0)


def gather_kernel(count, in_ref, out_ref, send_sem, recv_sem):
    me = lax.axis_index("sub")
    barrier = pltpu.get_barrier_semaphore()
    for step in range(1, count):
        pl.semaphore_signal(
            barrier,
            inc=1,
            device_id={"sub": lax.rem(me + step, count)},
            device_id_type=pl.DeviceIdType.MESH,
        )
    pl.semaphore_wait(barrier, count - 1)
    copies = []
    for step in range(1, count):
        copy = pltpu.make_async_remote_copy(
            src_ref=in_ref,
            dst_ref=out_ref.at[me],
            send_sem=send_sem.at[step - 1],
            recv_sem=recv_sem.at[step - 1],
            device_id={"sub": lax.rem(me + step, count)},
            device_id_type=pl.DeviceIdType.MESH,
        )
        copy.start()
        copies.append(copy)
    out_ref[pl.ds(me, 1)] = in_ref[...][None]
    for copy in copies:
        copy.wait()


def gather_tables(table, count):
    return pl.pallas_call(
        functools.partial(gather_kernel, count),
        out_shape=jax.ShapeDtypeStruct((count,) + table.shape, table.dtype),
        in_specs=[pl.BlockSpec(memory_space=pltpu.VMEM)],
        out_specs=pl.BlockSpec(memory_space=pltpu.VMEM),
        scratch_shapes=[
            pltpu.SemaphoreType.DMA((count - 1,)),
            pltpu.SemaphoreType.DMA((count - 1,)),
        ],
        compiler_params=pltpu.CompilerParams(collective_id=0, has_side_effects=True),
    )(table)


def solve_kernel(
    share, levels, gases, chunk, unroll,
    base_ref, flag_ref, gas_hbm, mass_hbm, state_hbm, coef_ref, omega_ref, weight_ref,
    heat_ref, down_ref,
    gas, mass, state, wide, half, weight, passing, direct, inverse, albedo, net, sems,
):
    gpoints, columns = half.shape
    base = base_ref[0]

    def fetch(j):
        return (
            pltpu.make_async_copy(gas_hbm.at[base + j], gas.at[j], sems.at[0, j]),
            pltpu.make_async_copy(mass_hbm.at[base + j], mass.at[j], sems.at[1, j]),
            pltpu.make_async_copy(state_hbm.at[base + j], state.at[j], sems.at[2, j]),
        )

    def start(j, carry):
        for copy in fetch(j):
            copy.start()
        return carry

    lax.fori_loop(0, share, start, 0)
    half[...] = jnp.broadcast_to(0.5 * omega_ref[...], half.shape)
    weight[...] = jnp.broadcast_to(weight_ref[...], weight.shape)
    lane = lax.broadcasted_iota(jnp.int32, (gpoints, chunk * gases), 1) // gases
    table = coef_ref[...].astype(jnp.float32)
    for i in range(chunk):
        wide[i * gpoints : (i + 1) * gpoints, :] = jnp.where(
            lane == chunk - 1 - i, table, 0.0
        ).astype(jnp.bfloat16)

    def solve(j, carry):
        for copy in fetch(j):
            copy.wait()

        @pl.when(flag_ref[j] == 1)
        def _():
            own = state[j].astype(jnp.float32)
            cosine = own[0:1, :]
            ground = own[1:2, :]
            scale = jnp.broadcast_to(1.0 / cosine, (8, columns))
            scale = jnp.concatenate([scale] * (gpoints // 8), axis=0)

            def upward(step, lower):
                first = levels - (step + 1) * chunk
                rows = gas[j, pl.ds(pl.multiple_of(first * gases, chunk * gases), chunk * gases), :]
                optical = jnp.dot(wide[...], rows, preferred_element_type=jnp.float32)
                for i in range(chunk):
                    layer = first + (chunk - 1 - i)
                    power = optical[i * gpoints : (i + 1) * gpoints] * (-LOG2E)
                    passed = jnp.exp2(power)
                    passing[layer] = passed
                    direct[layer] = jnp.exp2(power * scale)
                    squared = passed * passed
                    reflected = half[...] * (1.0 - squared)
                    rate = 1.0 / (1.0 - reflected * lower)
                    inverse[layer] = rate
                    lower = reflected + squared * (lower * rate)
                    albedo[layer] = lower
                return lower

            lax.fori_loop(
                0, levels // chunk, upward, jnp.broadcast_to(ground, (gpoints, columns))
            )

            def total(x):
                return jnp.sum(x.reshape(gpoints // 8, 8, columns), axis=0)

            def downward(step, carry):
                beam, diffuse = carry
                for i in range(unroll):
                    layer = step * unroll + i
                    net[layer] = total((1.0 - albedo[layer]) * (beam + diffuse))
                    after = beam * direct[layer]
                    diffuse = (
                        passing[layer] * diffuse + half[...] * (beam - after)
                    ) * inverse[layer]
                    beam = after
                return beam, diffuse

            beam, diffuse = lax.fori_loop(
                0,
                levels // unroll,
                downward,
                (weight[...] * cosine, jnp.zeros((gpoints, columns), jnp.float32)),
            )
            bottom = total(beam + diffuse)
            net[levels] = (1.0 - ground) * bottom
            change = jnp.sum(net[0:levels] - net[1 : levels + 1], axis=1)
            heat_ref[j] = mass[j].astype(jnp.float32) * change
            down_ref[pl.ds(j, 1), :] = jnp.sum(bottom, axis=0, keepdims=True)

        @pl.when(flag_ref[j] != 1)
        def _():
            heat_ref[j] = jnp.zeros((levels, columns), jnp.float32)
            down_ref[pl.ds(j, 1), :] = jnp.zeros((1, columns), jnp.float32)

        return carry

    lax.fori_loop(0, share, solve, 0)


def body(gas_amounts, layer_mass, column_state, absorption, single_scatter, solar_weight, sunlit):
    sub_count = lax.axis_size("sub")
    owned, levels, gases, columns = gas_amounts.shape
    share = owned // sub_count
    local = absorption.shape[0]
    gpoints = local * sub_count
    base = lax.axis_index("sub") * share
    flags = lax.dynamic_slice_in_dim(sunlit, lax.axis_index("band") * owned + base, share)
    table = jnp.concatenate(
        [
            absorption.astype(jnp.float32),
            single_scatter[:, None],
            solar_weight[:, None],
        ],
        axis=1,
    )
    table = jnp.pad(table, ((0, -local % 8), (0, 128 - gases - 2)))
    gathered = gather_tables(table, sub_count)[:, :local].reshape(gpoints, 128)
    chunk = 128 // gases
    coefficients = jnp.tile(gathered[:, :gases].astype(jnp.bfloat16), (1, chunk))
    omega = gathered[:, gases : gases + 1]
    weight = gathered[:, gases + 1 : gases + 2]
    smem = pl.BlockSpec(memory_space=pltpu.SMEM)
    vmem = pl.BlockSpec(memory_space=pltpu.VMEM)
    hbm = pl.BlockSpec(memory_space=pl.ANY)
    f32 = jnp.float32
    return pl.pallas_call(
        functools.partial(solve_kernel, share, levels, gases, chunk, 4),
        out_shape=(
            jax.ShapeDtypeStruct((share, levels, columns), f32),
            jax.ShapeDtypeStruct((share, columns), f32),
        ),
        in_specs=[smem, smem, hbm, hbm, hbm, vmem, vmem, vmem],
        out_specs=(vmem, vmem),
        scratch_shapes=[
            pltpu.VMEM((share, levels * gases, columns), jnp.bfloat16),
            pltpu.VMEM((share, levels, columns), jnp.bfloat16),
            pltpu.VMEM((share, 2, columns), jnp.bfloat16),
            pltpu.VMEM((chunk * gpoints, chunk * gases), jnp.bfloat16),
            pltpu.VMEM((gpoints, columns), f32),
            pltpu.VMEM((gpoints, columns), f32),
            pltpu.VMEM((levels, gpoints, columns), f32),
            pltpu.VMEM((levels, gpoints, columns), f32),
            pltpu.VMEM((levels, gpoints, columns), f32),
            pltpu.VMEM((levels, gpoints, columns), f32),
            pltpu.VMEM((levels + 1, 8, columns), f32),
            pltpu.SemaphoreType.DMA((3, share)),
        ],
        compiler_params=pltpu.CompilerParams(vmem_limit_bytes=48 * 1024 * 1024),
    )(
        base.reshape(1).astype(jnp.int32),
        flags,
        gas_amounts.reshape(owned, levels * gases, columns),
        layer_mass,
        column_state,
        coefficients,
        omega,
        weight,
    )


def solution(mesh):
    in_specs = (
        P("band", None, None, None),
        P("band", None, None),
        P("band", None, None),
        P("sub", None),
        P("sub"),
        P("sub"),
        P(),
    )
    out_specs = (P(("band", "sub"), None, None), P(("band", "sub"), None))
    return jax.shard_map(body, mesh=mesh, in_specs=in_specs, out_specs=out_specs, check_vma=False)
```

time: 543 us -> 80.5 us (0.15)
  other arithmetic: 253 us -> 0.69 us
  local copies, waits for them, and re-layouts: 145 us -> 6.15 us
  Pallas kernels: 0 us -> 72.5 us
  waiting for transfers between devices: 66.6 us -> 0 us
  blocking collectives: 22.8 us -> 0 us
  starting transfers between devices: 22.6 us -> 0 us
  between operations: 15 us -> 0.67 us
  matrix products: 11.6 us -> 0 us
    while x64 -> x0, other arithmetic: 96.9 us -> none
    pallas_call x0 -> x2, Pallas kernels: none -> 72.6 us  [the longest x1 65.1 us: body(): pl.pallas_call(functools.partial(solve_kernel, share, levels, gases, chun...]
    neg x2 -> x0, local copies, waits for them, and re-layouts: 59.6 us -> none  [layer_solve(): passing = jnp.exp(-optical)]
    reduce_scatter x2 -> x0, waiting for transfers between devices: 52.1 us -> none  [the longest x1 44.7 us: body(): lax.psum_scatter(heat_own, 'sub', scatter_dimension=0, tiled=True)]
    reduce_sum x20 -> x0, other arithmetic: 50.9 us -> none  [the longest x16 49.8 us: downward(): return ((new_beam, new_diffuse), jnp.sum(net_flux, axis=0))]
    div x16 -> x0, other arithmetic: 47.4 us -> none  [downward(): (pass_now * diffuse + 0.5 * omega * (1.0 - direct_now) * beam) / denominator]
    dynamic_update_slice x16 -> x0, local copies, waits for them, and re-layouts: 40.1 us -> none  [the longest x8 35.2 us: layer_solve(): lax.scan(upward, surface, (reflected, passing), reverse=True, unroll=8)]
    mul x12 -> x0, other arithmetic: 40 us -> none  [the longest x2 39.1 us: layer_solve(): reflected = 0.5 * omega * (1.0 - passing * passing)]
  transfers between devices with their start and end apart: 7 -> 0, of which waited for: 5 -> 0; matrix products, arithmetic and copies ran while one was open for 4% -> 0% of each run, Pallas kernels for 0% -> 0%
where the time goes in v1:
time: 80.5 us; the launch traced here: 80.1 us
  Pallas kernels  72.5 us (90%)
  local copies, waits for them, and re-layouts  6.15 us (8%)
    pallas_call x1, Pallas kernels, body(): pl.pallas_call(functools.partial(solve_kernel, share, levels, gases, chun...  65.1 us
    pallas_call x1, Pallas kernels, gather_tables(): pl.pallas_call(functools.partial(gather_kernel, count), out_shape=jax.Sha...  7.5 us
    unnamed x4, local copies, waits for them, and re-layouts  1.98 us

profile of v1, /device:TPU:2, one launch (start us, length us, event | category | flops | bytes accessed | tf_op | source)
XLA Modules:
  0.0 80.1 jit_solution(15855830042612299625)
XLA Ops:
  0.6 0.8 dynamic_slice.3.flag_ref
  1.4 0.8 copy.17
  2.2 0.7 copy.18
  2.9 0.7 copy.19
  3.7 0.7 select_maximum_fusion.in_ref
  4.3 7.5 %shard_map.86 = f32[4,32,128]{2,1,0:T(8,128)} custom-call(f32[32,128]{1,0:T(8,128)} %select_maximum_fusion.in_ref), custom_call_target="tpu_custom_call" | custom-call | tf_op jit(solution)/shard_map/pallas_call | solution.py:43
  11.9 0.8 %reshape.19 = f32[112,128]{1,0:T(8,128)S(1)} reshape(f32[4,28,128]{2,1,0:T(8,128)} %bitcast.8) | data formatting | bytes 114688 | tf_op jit(solution)/shard_map/reshape | solution.py:175
  12.7 0.1 copy.20
  12.8 0.1 copy.21.coef_ref
  12.9 0.1 fusion
  13.0 0.0 copy-start
  13.0 1.2 %copy-done = bf16[64,64,128]{2,1,0:T(8,128)(2,1)S(1)} copy-done((bf16[64,64,128]{2,1,0:T(8,128)(2,1)S(1)}, bf16[64,64,128]{2,1,0:T(8,128)(2,1)}, u32[]{:S(2)}) %copy-start) | copy-done | bytes 1048600
  14.2 0.0 copy-start.1
  14.2 0.8 copy-done.1
  15.0 65.1 %shard_map.87 = (f32[16,64,128]{2,1,0:T(8,128)}, f32[16,128]{1,0:T(8,128)}) custom-call(s32[1]{0:T(128)} %bitcast.base_ref, s32[16]{0:T(128)S(1)} %dynamic_slice.3.flag_ref, bf16[64,512,128]{2,1,0:T(8,128)(2,1)} %bitcast.7, bf16[64,64,128]{2,1,0:T(8,128)(2,1)S(1)} %copy-done, bf16[64,2,128]{2,1,0:T(2,128)(2,1)S(1)} %copy-done.1, ...), custom_call_target="tpu_custom_call" | custom-call | tf_op jit(solution)/shard_map/pallas_call | solution.py:184
  (2 shorter events, 0.0 us)
Async XLA Ops:
  13.0 1.2 %copy-start = (bf16[64,64,128]{2,1,0:T(8,128)(2,1)S(1)}, bf16[64,64,128]{2,1,0:T(8,128)(2,1)}, u32[]{:S(2)}) copy-start(bf16[64,64,128]{2,1,0:T(8,128)(2,1)} %mass_hbm.1) | copy-start | bytes 3145732
  14.2 0.8 copy-start.1

commit v2 on v1

--- a/solution.py
+++ b/solution.py
@@ -55,12 +55,13 @@
 
 def solve_kernel(
     share, levels, gases, chunk, unroll,
-    base_ref, flag_ref, gas_hbm, mass_hbm, state_hbm, coef_ref, omega_ref, weight_ref,
+    flag_ref, gas_hbm, mass_hbm, state_hbm, tables_ref,
     heat_ref, down_ref,
-    gas, mass, state, wide, half, weight, passing, direct, inverse, albedo, net, sems,
+    gas, mass, state, table, wide, half, weight, passing, direct, inverse, albedo, net, sems,
 ):
     gpoints, columns = half.shape
-    base = base_ref[0]
+    base = lax.axis_index("sub") * share
+    first_flag = lax.axis_index("band") * gas_hbm.shape[0] + base
 
     def fetch(j):
         return (
@@ -75,20 +76,32 @@
         return carry
 
     lax.fori_loop(0, share, start, 0)
-    half[...] = jnp.broadcast_to(0.5 * omega_ref[...], half.shape)
-    weight[...] = jnp.broadcast_to(weight_ref[...], weight.shape)
-    lane = lax.broadcasted_iota(jnp.int32, (gpoints, chunk * gases), 1) // gases
-    table = coef_ref[...].astype(jnp.float32)
+    subs, rows, lanes = tables_ref.shape
+    local = gpoints // subs
+    blank = jnp.zeros((lanes - rows, lanes), jnp.float32)
+    for s in range(subs):
+        turned = jnp.concatenate([tables_ref[s], blank], axis=0).T
+        table[s * local : (s + 1) * local, :] = turned[:local]
+    full = table[...]
+    half[...] = jnp.broadcast_to(0.5 * full[:, gases : gases + 1], half.shape)
+    weight[...] = jnp.broadcast_to(full[:, gases + 1 : gases + 2], weight.shape)
+    lane = lax.broadcasted_iota(jnp.int32, (gpoints, lanes), 1)
+    spread = jnp.where(lane < gases, full, 0.0)
+    width = gases
+    while width < lanes:
+        spread = spread + pltpu.roll(spread, width, 1)
+        width *= 2
+    lane = lane // gases
     for i in range(chunk):
         wide[i * gpoints : (i + 1) * gpoints, :] = jnp.where(
-            lane == chunk - 1 - i, table, 0.0
+            lane == chunk - 1 - i, spread, 0.0
         ).astype(jnp.bfloat16)
 
     def solve(j, carry):
         for copy in fetch(j):
             copy.wait()
 
-        @pl.when(flag_ref[j] == 1)
+        @pl.when(flag_ref[first_flag + j] == 1)
         def _():
             own = state[j].astype(jnp.float32)
             cosine = own[0:1, :]
@@ -145,7 +158,7 @@
             heat_ref[j] = mass[j].astype(jnp.float32) * change
             down_ref[pl.ds(j, 1), :] = jnp.sum(bottom, axis=0, keepdims=True)
 
-        @pl.when(flag_ref[j] != 1)
+        @pl.when(flag_ref[first_flag + j] != 1)
         def _():
             heat_ref[j] = jnp.zeros((levels, columns), jnp.float32)
             down_ref[pl.ds(j, 1), :] = jnp.zeros((1, columns), jnp.float32)
@@ -161,25 +174,20 @@
     share = owned // sub_count
     local = absorption.shape[0]
     gpoints = local * sub_count
-    base = lax.axis_index("sub") * share
-    flags = lax.dynamic_slice_in_dim(sunlit, lax.axis_index("band") * owned + base, share)
     table = jnp.concatenate(
         [
-            absorption.astype(jnp.float32),
-            single_scatter[:, None],
-            solar_weight[:, None],
+            absorption.T.astype(jnp.float32),
+            single_scatter[None, :],
+            solar_weight[None, :],
         ],
-        axis=1,
+        axis=0,
     )
-    table = jnp.pad(table, ((0, -local % 8), (0, 128 - gases - 2)))
-    gathered = gather_tables(table, sub_count)[:, :local].reshape(gpoints, 128)
+    table = jnp.pad(table, ((0, -(gases + 2) % 8), (0, 128 - local)))
+    gathered = gather_tables(table, sub_count)
     chunk = 128 // gases
-    coefficients = jnp.tile(gathered[:, :gases].astype(jnp.bfloat16), (1, chunk))
-    omega = gathered[:, gases : gases + 1]
-    weight = gathered[:, gases + 1 : gases + 2]
     smem = pl.BlockSpec(memory_space=pltpu.SMEM)
     vmem = pl.BlockSpec(memory_space=pltpu.VMEM)
-    hbm = pl.BlockSpec(memory_space=pl.ANY)
+    hbm = pl.BlockSpec(memory_space=pltpu.HBM)
     f32 = jnp.float32
     return pl.pallas_call(
         functools.partial(solve_kernel, share, levels, gases, chunk, 4),
@@ -187,12 +195,13 @@
             jax.ShapeDtypeStruct((share, levels, columns), f32),
             jax.ShapeDtypeStruct((share, columns), f32),
         ),
-        in_specs=[smem, smem, hbm, hbm, hbm, vmem, vmem, vmem],
+        in_specs=[smem, hbm, hbm, hbm, vmem],
         out_specs=(vmem, vmem),
         scratch_shapes=[
             pltpu.VMEM((share, levels * gases, columns), jnp.bfloat16),
             pltpu.VMEM((share, levels, columns), jnp.bfloat16),
             pltpu.VMEM((share, 2, columns), jnp.bfloat16),
+            pltpu.VMEM((gpoints, 128), f32),
             pltpu.VMEM((chunk * gpoints, chunk * gases), jnp.bfloat16),
             pltpu.VMEM((gpoints, columns), f32),
             pltpu.VMEM((gpoints, columns), f32),
@@ -203,16 +212,13 @@
             pltpu.VMEM((levels + 1, 8, columns), f32),
             pltpu.SemaphoreType.DMA((3, share)),
         ],
-        compiler_params=pltpu.CompilerParams(vmem_limit_bytes=48 * 1024 * 1024),
+        compiler_params=pltpu.CompilerParams(vmem_limit_bytes=66000000),
     )(
-        base.reshape(1).astype(jnp.int32),
-        flags,
+        sunlit,
         gas_amounts.reshape(owned, levels * gases, columns),
         layer_mass,
         column_state,
-        coefficients,
-        omega,
-        weight,
+        gathered,
     )
 
 

time: 80.5 us -> 74.3 us (0.923)
  the two profiles are of different devices: /device:TPU:2 before, /device:TPU:24 now
where the time goes in v2:
time: 74.3 us; the launch traced here: 73 us
  Pallas kernels  70.4 us (95%)
  other arithmetic  1.96 us (3%)
    pallas_call x1, Pallas kernels, body(): pl.pallas_call(functools.partial(solve_kernel, share, levels, gases, chun...  63.4 us
    pallas_call x1, Pallas kernels, gather_tables(): pl.pallas_call(functools.partial(gather_kernel, count), out_shape=jax.Sha...  6.97 us

profile of v2, /device:TPU:24, one launch (start us, length us, event | category | flops | bytes accessed | tf_op | source)
XLA Modules:
  0.0 73.0 jit_solution(13052155400258063856)
XLA Ops:
  0.6 0.7 convert_bitcast_fusion
  1.3 1.3 %select_maximum_fusion.in_ref = f32[16,128]{1,0:T(8,128)} fusion(f32[1,28]{1,0:T(1,128)} %bitcast.6, f32[1,28]{1,0:T(1,128)} %bitcast.7, f32[8,28]{1,0:T(8,128)S(1)} %convert_bitcast_fusion), kind=kLoop, calls=%fused_computation | loop fusion | flops 22528 | bytes 9312 | tf_op jit(solution)/shard_map/concatenate | solution.py:177
  2.6 7.0 %shard_map.86.tables_ref = f32[4,16,128]{2,1,0:T(8,128)} custom-call(f32[16,128]{1,0:T(8,128)} %select_maximum_fusion.in_ref), custom_call_target="tpu_custom_call" | custom-call | tf_op jit(solution)/shard_map/pallas_call | solution.py:43
  9.6 63.4 %shard_map.87 = (f32[16,64,128]{2,1,0:T(8,128)}, f32[16,128]{1,0:T(8,128)}) custom-call(s32[512]{0:T(512)} %flag_ref.1, bf16[64,512,128]{2,1,0:T(8,128)(2,1)} %bitcast.5, bf16[64,64,128]{2,1,0:T(8,128)(2,1)} %mass_hbm.1, bf16[64,2,128]{2,1,0:T(2,128)(2,1)} %state_hbm.1, f32[4,16,128]{2,1,0:T(8,128)} %shard_map.86.tables_ref), custom_call_target="tpu_custom_call" | custom-call | tf_op jit(solution)/shard_map/pallas_call | solution.py:192
